TPU v7x, 32 devices: a whole 2x2x4 slice. The times are simulated.
32 devices in a mesh: dp: 4 (over y, x), context: 4 (over z), head: 2 (over core).
Axes of the slice: x: 2, y: 2, z: 4, core: 2. Of those that a mesh axis runs over, the one named last changes fastest.
Arguments:
- tokens: bfloat16 [4, 2, 512, 4096], P('dp', None, 'context', 'head'), may hold values from -7 to 7
- queries: bfloat16 [4, 2, 512, 2048], P('dp', None, 'context', 'head'), may hold values from -160 to 160
- grad_out: bfloat16 [4, 2, 512, 2048], P('dp', None, 'context', 'head'), may hold values from -6 to 6
- w_key: bfloat16 [4096, 256], P('context', 'head'), may hold values from -0.09375 to 0.09375
- w_value: bfloat16 [4096, 256], P('context', 'head'), may hold values from -0.09375 to 0.09375
- block_len: int32 [4], P('dp'), may hold values from 8 to 32, as said below
Outputs:
- grad_query: bfloat16 [4, 2, 512, 2048], P('dp', None, 'context', 'head')
- grad_x: bfloat16 [4, 2, 512, 4096], P('dp', None, 'context', 'head')
- grad_wkey: float32 [4096, 256], P('context', 'head')
- grad_wvalue: float32 [4096, 256], P('context', 'head')
Inputs may be any that keep to these rules, and one draw needn't show every extreme that they name: `block_len`: each entry is 8, 16 or 32.
All inputs are finite; a program needn't handle non-finite values.
Results may differ from a plain program's by a relative error of at most 0.025.
Values may be sent and summed in bfloat16 or wider, within the bound.
A program may use at most 64 MiB of HBM per device.

v0:
```python
import math
import jax
import jax.numpy as jnp
from jax import lax
from jax.sharding import PartitionSpec as P

HEAD_DIM = 128
masked_score = -1e30


def score_block(query_rows, key_rows, score_scale):
    return (
        jnp.einsum("ikgd,jkd->kgij", query_rows, key_rows, preferred_element_type=jnp.float32)
        * score_scale
    )


def visible_mask(query_pos, key_pos, block_size, strict):
    query_block = query_pos // block_size
    key_block = key_pos // block_size
    if strict:
        return key_block[None, :] < query_block[:, None]
    return key_block[None, :] <= query_block[:, None]


def forward_step(carried, query_rows, key_rows, value_rows, allowed_mask, score_scale):
    row_peak, row_total, weighted = carried
    logits = jnp.where(allowed_mask, score_block(query_rows, key_rows, score_scale), masked_score)
    new_peak = jnp.maximum(row_peak, jnp.max(logits, axis=-1))
    shrink = jnp.exp(row_peak - new_peak)
    weights = jnp.where(allowed_mask, jnp.exp(logits - new_peak[..., None]), 0.0)
    row_total = row_total * shrink + jnp.sum(weights, axis=-1)
    update = jnp.einsum(
        "kgij,jkd->kgid",
        weights.astype(jnp.bfloat16),
        value_rows,
        preferred_element_type=jnp.float32,
    )
    return (new_peak, row_total, weighted * shrink[..., None] + update)


def backward_step(
    query_rows, grad_rows, key_rows, value_rows, allowed_mask, log_total, row_delta, score_scale
):
    logits = jnp.where(allowed_mask, score_block(query_rows, key_rows, score_scale), masked_score)
    probs = jnp.exp(logits - log_total[..., None])
    probs_half = probs.astype(jnp.bfloat16)
    grad_probs = jnp.einsum(
        "ikgd,jkd->kgij", grad_rows, value_rows, preferred_element_type=jnp.float32
    )
    grad_logits = (probs * (grad_probs - row_delta[..., None])).astype(jnp.bfloat16)
    grad_rows_query = jnp.einsum(
        "kgij,jkd->ikgd", grad_logits, key_rows, preferred_element_type=jnp.float32
    )
    grad_key = (
        jnp.einsum("kgij,ikgd->jkd", grad_logits, query_rows, preferred_element_type=jnp.float32)
        * score_scale
    )
    grad_value = jnp.einsum(
        "kgij,ikgd->jkd", probs_half, grad_rows, preferred_element_type=jnp.float32
    )
    return (grad_rows_query, grad_key, grad_value)


def finish_rows(carried, grad_rows):
    row_peak, row_total, weighted = carried
    outputs = weighted / row_total[..., None]
    row_delta = jnp.einsum("ikgd,kgid->kgi", grad_rows.astype(jnp.float32), outputs)
    return (row_peak + jnp.log(row_total), row_delta)


def per_device(tokens, queries, grad_out, w_key, w_value, block_len):
    cycle_size = lax.axis_size("context")
    my_index = lax.axis_index("context")
    shard_rows = tokens.shape[2]
    kv_width = w_key.shape[1]
    kv_local = kv_width // HEAD_DIM
    query_width = queries.shape[3]
    group_size = query_width // HEAD_DIM // kv_local
    score_scale = 1.0 / math.sqrt(HEAD_DIM)
    block_size = block_len[0]
    local_pos = lax.iota(jnp.int32, shard_rows)
    span_rows = min(cycle_size * shard_rows, max(512, shard_rows))
    full_tokens = lax.all_gather(
        tokens[0].reshape(2 * shard_rows, tokens.shape[3]), "head", axis=1, tiled=True
    )
    weight_pair = jnp.concatenate([w_key, w_value], axis=1)
    columns = full_tokens
    projected = jnp.dot(
        columns,
        lax.all_gather(weight_pair, "context", axis=0, tiled=True),
        preferred_element_type=jnp.float32,
    ).astype(jnp.bfloat16)
    clean_pairs = projected[:shard_rows]
    q_clean = queries[0, 0].reshape(shard_rows, kv_local, group_size, HEAD_DIM)
    g_clean = grad_out[0, 0].reshape(shard_rows, kv_local, group_size, HEAD_DIM)
    noisy_bundle = jnp.concatenate([queries[0, 1], grad_out[0, 1], projected[shard_rows:]], axis=1)
    q_noisy = noisy_bundle[:, :query_width].reshape(shard_rows, kv_local, group_size, HEAD_DIM)
    g_noisy = noisy_bundle[:, query_width : 2 * query_width].reshape(
        shard_rows, kv_local, group_size, HEAD_DIM
    )
    k_noisy = noisy_bundle[:, 2 * query_width : 2 * query_width + kv_width].reshape(
        shard_rows, kv_local, HEAD_DIM
    )
    v_noisy = noisy_bundle[:, 2 * query_width + kv_width :].reshape(shard_rows, kv_local, HEAD_DIM)
    clean_pos = my_index * shard_rows + local_pos
    noisy_pos = my_index * shard_rows + local_pos
    own_block = local_pos // block_size
    same_block = own_block[None, :] == own_block[:, None]
    clean_limit = (my_index + 1) * shard_rows
    noisy_limit = (my_index + 1) * shard_rows
    state_shape = (kv_local, group_size, shard_rows)
    empty_state = (
        jnp.full(state_shape, masked_score, jnp.float32),
        jnp.zeros(state_shape, jnp.float32),
        jnp.zeros(state_shape + (HEAD_DIM,), jnp.float32),
    )
    noisy_start = forward_step(empty_state, q_noisy, k_noisy, v_noisy, same_block, score_scale)
    block_turns = (jnp.maximum(clean_limit, noisy_limit) + span_rows - 1) // span_rows

    def split_pairs(pair_rows):
        count_rows = pair_rows.shape[0]
        key_rows = pair_rows[:, :kv_width].reshape(count_rows, kv_local, HEAD_DIM)
        value_rows = pair_rows[:, kv_width:].reshape(count_rows, kv_local, HEAD_DIM)
        return (key_rows, value_rows)

    carried = (empty_state, noisy_start)
    pair_rows = lax.all_gather(clean_pairs, "context", axis=0, tiled=True)
    first_row = jnp.int32(0)
    key_rows, value_rows = split_pairs(pair_rows)
    key_pos = lax.iota(jnp.int32, pair_rows.shape[0])
    clean_mask = visible_mask(clean_pos, key_pos, block_size, False)
    noisy_mask = visible_mask(noisy_pos, key_pos, block_size, True)

    def clean_update():
        return forward_step(carried[0], q_clean, key_rows, value_rows, clean_mask, score_scale)

    def clean_keep():
        return carried[0]

    def noisy_update():
        return forward_step(carried[1], q_noisy, key_rows, value_rows, noisy_mask, score_scale)

    def noisy_keep():
        return carried[1]

    clean_state = lax.cond(first_row < clean_limit, clean_update, clean_keep)
    noisy_state = lax.cond(first_row < noisy_limit, noisy_update, noisy_keep)
    clean_lse, clean_delta = finish_rows(clean_state, g_clean)
    noisy_lse, noisy_delta = finish_rows(noisy_state, g_noisy)
    pairs_back = lax.all_gather(clean_pairs, "context", axis=0, tiled=True)
    query_zero = jnp.zeros((shard_rows, kv_local, group_size, HEAD_DIM), jnp.float32)

    def backward_turn(turn_index, carried):
        query_grads, pair_total = carried
        first_row = turn_index * span_rows
        pair_rows = lax.dynamic_slice_in_dim(pairs_back, first_row, span_rows, 0)
        key_rows, value_rows = split_pairs(pair_rows)
        key_pos = first_row + lax.iota(jnp.int32, span_rows)
        clean_mask = visible_mask(clean_pos, key_pos, block_size, False)
        noisy_mask = visible_mask(noisy_pos, key_pos, block_size, True)
        pair_zero = jnp.zeros((span_rows, kv_local, HEAD_DIM), jnp.float32)

        def clean_work():
            return backward_step(
                q_clean,
                g_clean,
                key_rows,
                value_rows,
                clean_mask,
                clean_lse,
                clean_delta,
                score_scale,
            )

        def noisy_work():
            return backward_step(
                q_noisy,
                g_noisy,
                key_rows,
                value_rows,
                noisy_mask,
                noisy_lse,
                noisy_delta,
                score_scale,
            )

        def no_work():
            return (query_zero, pair_zero, pair_zero)

        clean_dq, clean_dk, clean_dv = lax.cond(first_row < clean_limit, clean_work, no_work)
        noisy_dq, noisy_dk, noisy_dv = lax.cond(first_row < noisy_limit, noisy_work, no_work)
        pair_grads = jnp.concatenate(
            [
                (clean_dk + noisy_dk).reshape(span_rows, kv_width),
                (clean_dv + noisy_dv).reshape(span_rows, kv_width),
            ],
            axis=1,
        )
        previous = lax.dynamic_slice_in_dim(pair_total, first_row, span_rows, 0)
        pair_total = lax.dynamic_update_slice_in_dim(
            pair_total, previous + pair_grads, first_row, 0
        )
        return ((query_grads[0] + clean_dq, query_grads[1] + noisy_dq), pair_total)

    pair_empty = jnp.zeros((cycle_size * shard_rows, 2 * kv_width), jnp.float32)
    query_grads, pair_total = lax.fori_loop(
        0, block_turns, backward_turn, ((query_zero, query_zero), pair_empty)
    )
    clean_pair_grads = lax.psum_scatter(
        pair_total.astype(jnp.bfloat16), "context", scatter_dimension=0, tiled=True
    )
    own_dq, own_dk, own_dv = backward_step(
        q_noisy, g_noisy, k_noisy, v_noisy, same_block, noisy_lse, noisy_delta, score_scale
    )
    dq_clean = (query_grads[0] * score_scale).astype(jnp.bfloat16).reshape(shard_rows, query_width)
    dq_noisy = (
        ((query_grads[1] + own_dq) * score_scale)
        .astype(jnp.bfloat16)
        .reshape(shard_rows, query_width)
    )
    noisy_pair = jnp.concatenate(
        [own_dk.reshape(shard_rows, kv_width), own_dv.reshape(shard_rows, kv_width)], axis=1
    ).astype(jnp.bfloat16)
    return_bundle = jnp.concatenate([dq_noisy, noisy_pair], axis=1)
    dq_noisy = return_bundle[:, :query_width]
    noisy_pair = return_bundle[:, query_width:]
    pair_grads = jnp.concatenate([clean_pair_grads, noisy_pair], axis=0)
    input_terms = jnp.einsum(
        "tc,rc->tr",
        pair_grads,
        lax.all_gather(weight_pair, "context", axis=0, tiled=True),
        preferred_element_type=jnp.float32,
    )
    grad_x = lax.psum_scatter(
        input_terms.astype(jnp.bfloat16), "head", scatter_dimension=1, tiled=True
    ).reshape(tokens.shape)
    columns = full_tokens
    weight_local = lax.psum_scatter(
        jnp.einsum("tr,tc->rc", columns, pair_grads, preferred_element_type=jnp.float32).astype(
            jnp.bfloat16
        ),
        "context",
        scatter_dimension=0,
        tiled=True,
    )
    weight_sums = lax.psum(weight_local, "dp").astype(jnp.float32)
    grad_query = jnp.stack([dq_clean, dq_noisy])[None]
    return (grad_query, grad_x, weight_sums[:, :kv_width], weight_sums[:, kv_width:])


def solution(mesh):
    placed = (
        P("dp", None, "context", "head"),
        P("dp", None, "context", "head"),
        P("dp", None, "context", "head"),
        P("context", "head"),
        P("context", "head"),
        P("dp"),
    )
    return jax.shard_map(
        per_device,
        mesh=mesh,
        in_specs=placed,
        out_specs=(
            P("dp", None, "context", "head"),
            P("dp", None, "context", "head"),
            P("context", "head"),
            P("context", "head"),
        ),
        check_vma=False,
    )
```

profile of v0, /device:TPU:0, one launch (start us, length us, event | category | flops | bytes accessed | tf_op | source)
XLA Modules:
  0.0 246.0 jit_solution(10116017296213389250)
XLA Ops:
  7.2 0.7 all-gather.5.cloned.1.call-update
  8.0 1.9 pad_maximum_fusion
  10.9 0.9 copy.91
  11.9 0.9 copy.89
  14.0 8.9 %all-gather.5.cloned.1.call-done = bf16[256,4096]{1,0:T(8,128)(2,1)} async-done(((bf16[256,2048]{1,0:T(8,128)(2,1)}), bf16[256,4096]{1,0:T(8,128)(2,1)}) %all-gather.5.cloned.1.call-update) | async-done | bytes 2097168 | tf_op jit(solution)/shard_map/all_gather | solution.py:84
  22.9 49.0 %all-gather.3.cloned.1.call-done = bf16[4096,256]{1,0:T(8,128)(2,1)} async-done(((bf16[1024,256]{1,0:T(8,128)(2,1)}), bf16[4096,256]{1,0:T(8,128)(2,1)}) %all-gather.3.cloned.1.call-update) | async-done | bytes 2097168 | tf_op jit(solution)/shard_map/all_gather | solution.py:91
  71.9 3.0 %fusion.88 = bf16[256,256]{0,1:T(8,128)(2,1)S(1)} fusion(bf16[4096,256]{1,0:T(8,128)(2,1)} %all-gather.3.cloned.1.call-done, bf16[256,4096]{1,0:T(8,128)(2,1)} %all-gather.5.cloned.1.call-done), kind=kOutput, calls=%fused_computation.128 | convolution fusion | flops 536936448 | bytes 4325376 | tf_op jit(solution)/shard_map/dot_general | solution.py:89
  74.9 13.4 %all_gather.13 = bf16[512,256]{0,1:T(8,128)(2,1)S(1)} all-gather(bf16[128,256]{0,1:T(8,128)(2,1)S(1)} %slice.67), channel_id=1, replica_groups=mesh['dp'=4,'context'=4,'head'=2] {'context'}, dimensions={0}, use_global_device_ids=true | all-gather | bytes 327680 | tf_op jit(solution)/shard_map/all_gather | solution.py:151
  88.3 0.8 copy.88
  89.1 0.7 slice_bitcast_fusion.2
  89.8 0.3 fusion.114
  90.2 0.6 copy-done.1
  90.8 0.3 fusion.78
  91.2 2.9 %conditional.4 = (f32[1,8,128]{2,1,0:T(8,128)S(1)}, f32[1,8,128]{2,1,0:T(8,128)S(1)}, f32[1,8,128,128]{3,2,1,0:T(8,128)S(1)}, f32[1,8,128]{2,1,0:T(8,128)S(1)}) conditional(s32[]{:T(128)} %convert_element_type.73, () %tuple.57, (s32[512]{0:T(512)S(1)}, s32[128,512]{0,1:T(8,128)S(1)}, bf16[512,1,128]{0,2,1:T(8,128)(2,1)S(1)}, ...), branch_computations={%region_0.1_spmd, %region_1.4_spmd} | conditional | flops 275452928 | bytes 7919648 | solution.py:147
  91.4 0.5 fusion.4
  91.9 0.5 fusion.6
  92.4 1.7 fusion.7
  94.1 0.6 copy-done.12
  94.7 0.2 divide_bitcast_fusion.1
  94.9 0.2 copy.113
  95.1 2.9 %conditional.5 = (f32[1,8,128]{2,1,0:T(8,128)S(1)}, f32[1,8,128]{2,1,0:T(8,128)S(1)}, f32[1,8,128,128]{3,2,1,0:T(8,128)S(1)}, f32[1,8,128]{2,1,0:T(8,128)S(1)}) conditional(s32[]{:T(128)} %convert_element_type.73, (f32[1,8,128]{2,1,0:T(8,128)S(1)}, f32[1,8,128]{2,1,0:T(8,128)S(1)}, f32[1,8,128,128]{3,2,1,0:T(8,128)S(1)}) %tuple.59, ...), branch_computations={%region_6.7_spmd, %region_7.10_spmd} | conditional | flops 275581952 | bytes 8460320 | solution.py:148
  95.3 0.5 fusion.23
  95.8 1.7 fusion.26
  97.5 0.5 fusion.25
  98.1 0.2 divide_bitcast_fusion
  98.3 0.2 copy.122
  98.5 0.2 copy-done.13
  99.0 0.8 broadcast_in_dim.123
  99.8 13.3 %while.20 = (s32[]{:T(128)}, f32[128,1,8,128]{3,0,2,1:T(8,128)}, f32[128,1,8,128]{3,0,2,1:T(8,128)S(1)}, f32[512,256]{1,0:T(8,128)S(1)}, s32[]{:T(128)}, /*index...) while((s32[]{:T(128)}, f32[128,1,8,128]{3,0,2,1:T(8,128)}, ...), condition=%wide.region_15.16_spmd.clone.clone, body=%wide.region_10.15_spmd.clone.clone.sunk | while | flops 1350440704 | bytes 32791988 | solution.py:207
  99.8 0.8 fusion.130
  100.6 0.8 add_select_fusion.3
  101.4 1.0 slice_bitcast_fusion.11
  102.4 4.5 %conditional.12 = (f32[128,1,8,128]{3,0,2,1:T(8,128)S(1)}, f32[512,1,128]{2,0,1:T(8,128)S(1)}, f32[512,1,128]{2,0,1:T(8,128)S(1)}) conditional(s32[]{:T(128)} %convert_element_type.129, () %tuple.125, (s32[512]{0:T(512)S(1)}, s32[128,512]{0,1:T(8,128)S(1)}, bf16[512,1,128]{2,0,1:T(8,128)(2,1)S(1)}, bf16[128,1,8,128]{3,0,2,1:T(8,128)(2,1)}, ...), branch_computations={%region_11.11_spmd, %region_12.12_spmd} | conditional | flops 674889728 | bytes 12331032 | solution.py:191
  102.6 1.5 fusion.45
  104.1 0.4 convolution_bitcast_fusion.2
  104.5 0.4 fusion.46
  105.0 1.4 fusion.48
  106.4 0.5 convolution_bitcast_fusion.1
  106.9 1.9 add.307
  108.8 4.0 %conditional.13 = (f32[128,1,8,128]{3,0,2,1:T(8,128)S(1)}, f32[512,1,128]{2,0,1:T(8,128)S(1)}, f32[512,1,128]{2,0,1:T(8,128)S(1)}) conditional(s32[]{:T(128)} %convert_element_type.129, () %tuple.127, (s32[512]{0:T(512)S(1)}, s32[128,512]{0,1:T(8,128)S(1)}, bf16[512,1,128]{2,0,1:T(8,128)(2,1)S(1)}, bf16[128,1,8,128]{3,0,2,1:T(8,128)(2,1)}, ...), branch_computations={%region_13.13_spmd, %region_14.14_spmd} | conditional | flops 674889728 | bytes 13379636 | solution.py:192
  108.9 1.5 fusion.61
  110.4 0.4 convolution_bitcast_fusion.5
  110.9 0.4 fusion.62
  111.3 0.5 copy-done.3
  111.8 0.4 fusion.64
  112.3 0.5 convolution_bitcast_fusion.4
  113.3 0.8 copy.131
  114.2 1.4 fusion.87
  115.6 0.2 fusion.91
  115.9 0.2 fusion.90
  116.1 16.7 %reduce-scatter.10.cloned.1.call-done = bf16[128,256]{1,0:T(8,128)(2,1)} async-done(((bf16[512,256]{1,0:T(8,128)(2,1)}), bf16[128,256]{1,0:T(8,128)(2,1)}) %reduce-scatter.10.cloned.1.call-update) | async-done | bytes 65552
  132.8 0.9 copy.132
  133.7 3.7 %fusion.77 = bf16[4096,256]{0,1:T(8,128)(2,1)} fusion(bf16[256,4096]{1,0:T(8,128)(2,1)} %all-gather.5.cloned.1.call-done, bf16[128,128]{0,1:T(8,128)(2,1)S(1)} %fusion.90, bf16[128,128]{0,1:T(8,128)(2,1)S(1)} %fusion.91, bf16[128,256]{0,1:T(8,128)(2,1)S(1)} %copy.132), kind=kOutput, calls=%fused_computation.112 | convolution fusion | flops 538312704 | bytes 4325376 | tf_op jit(solution)/shard_map/tr,tc->rc/dot_general | solution.py:240
  137.5 41.9 %reduce-scatter.8.cloned.1.call-done = bf16[1024,256]{0,1:T(8,128)(2,1)} async-done(((bf16[4096,256]{0,1:T(8,128)(2,1)}), bf16[1024,256]{0,1:T(8,128)(2,1)}) %reduce-scatter.8.cloned.1.call-update) | async-done | bytes 524304 | tf_op jit(solution)/shard_map/reduce_scatter | solution.py:239
  179.5 2.1 convolution_convert_fusion.1
  181.6 1.0 copy-done
  183.1 0.2 copy.97
  183.3 1.0 fusion.84
  184.4 0.8 maximum_bitcast_fusion
  185.2 41.6 %all-reduce.2.cloned.1.call-done = bf16[1024,256]{0,1:T(8,128)(2,1)} async-done(((bf16[1024,256]{0,1:T(8,128)(2,1)}), bf16[1024,256]{0,1:T(8,128)(2,1)}) %all-reduce.2.cloned.1.call-update) | async-done | bytes 524304 | tf_op jit(solution)/shard_map/psum | solution.py:247
  226.9 1.1 fusion.111
  228.0 1.0 copy.104
  229.0 1.0 copy.103
  230.0 9.2 %reduce-scatter.6.cloned.1.call-done = bf16[256,2048]{1,0:T(8,128)(2,1)} async-done(((bf16[256,4096]{1,0:T(8,128)(2,1)}), bf16[256,2048]{1,0:T(8,128)(2,1)}) %reduce-scatter.6.cloned.1.call-update) | async-done | bytes 1048592 | tf_op jit(solution)/shard_map/reduce_scatter | solution.py:235
  (79 shorter events, 3.9 us)
Async XLA Ops:
  7.2 3.5 %copy-start.9 = (bf16[1,2,128,1024]{3,2,1,0:T(8,128)(2,1)S(1)}, bf16[1,2,128,1024]{3,2,1,0:T(8,128)(2,1)}, u32[]{:S(2)}) copy-start(bf16[1,2,128,1024]{3,2,1,0:T(8,128)(2,1)} %param.17) | copy-start | bytes 1572868
  7.2 15.7 %all-gather.5.cloned.1.call-start = ((), (), s32[]{:S(2)}) async-start(), calls=%async_computation.4 | async-start | bytes 3145728 | tf_op jit(solution)/shard_map/all_gather | solution.py:84
  7.9 64.0 %all-gather.3.cloned.1.call-start = ((), (), s32[]{:S(2)}) async-start(), calls=%async_computation.3 | async-start | bytes 2621440 | tf_op jit(solution)/shard_map/all_gather | solution.py:91
  9.8 2.9 %copy-start.10 = (bf16[1,2,128,1024]{3,2,1,0:T(8,128)(2,1)S(1)}, bf16[1,2,128,1024]{3,2,1,0:T(8,128)(2,1)}, u32[]{:S(2)}) copy-start(bf16[1,2,128,1024]{3,2,1,0:T(8,128)(2,1)} %param.18) | copy-start | bytes 1572868
  9.9 122.9 %reduce-scatter.10.cloned.1.call-start = ((), (), s32[]{:S(2)}) async-start(), calls=%async_computation.8 | async-start | bytes 327680
  10.8 84.3 %copy-start.4 = (bf16[1,1,128,1024]{2,3,1,0:T(8,128)(2,1)}, bf16[1,1,128,1024]{2,3,1,0:T(8,128)(2,1)S(1)}, u32[]{:S(2)}) copy-start(bf16[1,1,128,1024]{2,3,1,0:T(8,128)(2,1)S(1)} %copy.135) | copy-start | bytes 786436
  13.0 85.9 %copy-start.6 = (bf16[1,1,128,1024]{2,3,1,0:T(8,128)(2,1)}, bf16[1,1,128,1024]{2,3,1,0:T(8,128)(2,1)S(1)}, u32[]{:S(2)}) copy-start(bf16[1,1,128,1024]{2,3,1,0:T(8,128)(2,1)S(1)} %copy.136) | copy-start | bytes 786436
  74.8 16.4 %copy-start.11 = (bf16[256,256]{0,1:T(8,128)(2,1)}, bf16[256,256]{0,1:T(8,128)(2,1)S(1)}, u32[]{:S(2)}) copy-start(bf16[256,256]{0,1:T(8,128)(2,1)S(1)} %fusion.88) | copy-start | bytes 393220
  90.1 0.8 copy-start.1
  94.1 0.6 copy-start.12
  94.1 0.6 copy-start.14
  98.0 0.7 copy-start.13
  98.1 0.7 copy-start.15
  110.9 1.0 copy-start.3
  113.1 2.5 %copy-start.5 = (bf16[1,1,128,1024]{2,3,1,0:T(8,128)(2,1)S(1)}, bf16[1,1,128,1024]{2,3,1,0:T(8,128)(2,1)}, u32[]{:S(2)}) copy-start(bf16[1,1,128,1024]{2,3,1,0:T(8,128)(2,1)} %copy-done.4) | copy-start | bytes 786436
  113.1 2.7 %copy-start.2 = (f32[1,8,128,128]{2,3,1,0:T(8,128)S(1)}, f32[1,8,128,128]{2,3,1,0:T(8,128)}, u32[]{:S(2)}) copy-start(f32[1,8,128,128]{2,3,1,0:T(8,128)} %copy-done.1) | copy-start | bytes 1572868
  113.1 2.7 %copy-start.7 = (bf16[1,1,128,1024]{2,3,1,0:T(8,128)(2,1)S(1)}, bf16[1,1,128,1024]{2,3,1,0:T(8,128)(2,1)}, u32[]{:S(2)}) copy-start(bf16[1,1,128,1024]{2,3,1,0:T(8,128)(2,1)} %copy-done.6) | copy-start | bytes 786436
  114.1 65.3 %reduce-scatter.8.cloned.1.call-start = ((), (), s32[]{:S(2)}) async-start(), calls=%async_computation.6 | async-start | bytes 2621440 | tf_op jit(solution)/shard_map/reduce_scatter | solution.py:239
  137.4 42.1 %copy-start.8 = (bf16[4096,256]{1,0:T(8,128)(2,1)S(1)}, bf16[4096,256]{1,0:T(8,128)(2,1)}, u32[]{:S(2)}) copy-start(bf16[4096,256]{1,0:T(8,128)(2,1)} %all-gather.3.cloned.1.call-done) | copy-start | bytes 6291460
  137.4 89.4 %all-reduce.2.cloned.1.call-start = ((), (), s32[]{:S(2)}) async-start(), calls=%async_computation.7 | async-start | bytes 1048576 | tf_op jit(solution)/shard_map/psum | solution.py:247
  179.4 59.7 %reduce-scatter.6.cloned.1.call-start = ((), (), s32[]{:S(2)}) async-start(), calls=%async_computation.5 | async-start | bytes 3145728 | tf_op jit(solution)/shard_map/reduce_scatter | solution.py:235
  181.6 1.0 copy-start
Sparse Core Ops, SparseCore 0:
  9.5 13.2 all-gather.4
  25.0 46.8 all-gather.2
  114.3 18.4 reduce-scatter.9
  137.5 41.8 reduce-scatter.7
  182.3 44.5 all-reduce.1
  229.5 9.6 reduce-scatter.5
where the time goes:
time: 247 us; the launch traced here: 246 us
  waiting for transfers between devices  168 us (68%)
  matrix products  24.1 us (10%)
  local copies, waits for them, and re-layouts  15.5 us (6%)
  between operations  15.3 us (6%)
  blocking collectives  13.4 us (5%)
  other arithmetic  9.27 us (4%)
    all_gather x1, waiting for transfers between devices, per_device(): lax.all_gather(weight_pair, 'context', axis=0, tiled=True)  49 us
    reduce_scatter x1, waiting for transfers between devices, per_device(): lax.psum_scatter(jnp.einsum('tr,tc->rc', columns, pair_grads, preferred_e...  41.9 us
    psum x1, waiting for transfers between devices, per_device(): weight_sums = lax.psum(weight_local, 'dp').astype(jnp.float32)  41.6 us
    unnamed x7, waiting for transfers between devices  17.4 us
    all_gather x1, blocking collectives, per_device(): pairs_back = lax.all_gather(clean_pairs, 'context', axis=0, tiled=True)  13.4 us
    unnamed x45, local copies, waits for them, and re-layouts  10.3 us
    reduce_scatter x1, waiting for transfers between devices, per_device(): lax.psum_scatter(input_terms.astype(jnp.bfloat16), 'head', scatter_dimens...  9.19 us
    all_gather x1, waiting for transfers between devices, per_device(): lax.all_gather(tokens[0].reshape(2 * shard_rows, tokens.shape[3]), 'head'...  8.85 us
  transfers between devices with their start and end apart: 6, of which 6 were waited for; matrix products, arithmetic and copies ran while one was open for 6% of the time, Pallas kernels for 0%

commit v1 on v0

--- a/solution.py
+++ b/solution.py
@@ -6,6 +6,12 @@
 
 HEAD_DIM = 128
 masked_score = -1e30
+
+
+def summed_here(shard, axis):
+    terms = lax.all_gather(shard, axis, axis=0, tiled=False)
+    total = terms.sum(axis=0)
+    return total
 
 
 def score_block(query_rows, key_rows, score_scale):
@@ -244,7 +250,7 @@
         scatter_dimension=0,
         tiled=True,
     )
-    weight_sums = lax.psum(weight_local, "dp").astype(jnp.float32)
+    weight_sums = summed_here(weight_local, "dp").astype(jnp.float32)
     grad_query = jnp.stack([dq_clean, dq_noisy])[None]
     return (grad_query, grad_x, weight_sums[:, :kv_width], weight_sums[:, kv_width:])
 

time: 247 us -> 235 us (0.951)
  waiting for transfers between devices: 168 us -> 152 us
  other arithmetic: 9.27 us -> 12.1 us
    psum x1 -> x0, waiting for transfers between devices: 41.6 us -> none  [per_device(): weight_sums = lax.psum(weight_local, 'dp').astype(jnp.float32)]
    all_gather x0 -> x1, waiting for transfers between devices: none -> 30.3 us  [summed_here(): terms = lax.all_gather(shard, axis, axis=0, tiled=False)]
    reduce_scatter x1, waiting for transfers between devices: 9.19 us -> 4.04 us  [per_device(): lax.psum_scatter(input_terms.astype(jnp.bfloat16), 'head', scatter_dimens...]
    all_gather x0 -> x1, local copies, waits for them, and re-layouts: none -> 3.32 us  [summed_here(): terms = lax.all_gather(shard, axis, axis=0, tiled=False)]
    reduce_sum x0 -> x1, other arithmetic: none -> 2.85 us  [summed_here(): total = terms.sum(axis=0)]
  transfers between devices with their start and end apart: 6 -> 6, of which waited for: 6 -> 6; matrix products, arithmetic and copies ran while one was open for 6% -> 9% of each run, Pallas kernels for 0% -> 0%
where the time goes in v1:
time: 235 us
  waiting for transfers between devices  152 us (65%)
  matrix products  24.1 us (10%)
  local copies, waits for them, and re-layouts  17.8 us (8%)
  between operations  15.2 us (6%)
  blocking collectives  13.4 us (6%)
  other arithmetic  12.1 us (5%)
    all_gather x1, waiting for transfers between devices, per_device(): lax.all_gather(weight_pair, 'context', axis=0, tiled=True)  49 us
    reduce_scatter x1, waiting for transfers between devices, per_device(): lax.psum_scatter(jnp.einsum('tr,tc->rc', columns, pair_grads, preferred_e...  41.9 us
    all_gather x1, waiting for transfers between devices, summed_here(): terms = lax.all_gather(shard, axis, axis=0, tiled=False)  30.3 us
    unnamed x7, waiting for transfers between devices  17.4 us
    all_gather x1, blocking collectives, per_device(): pairs_back = lax.all_gather(clean_pairs, 'context', axis=0, tiled=True)  13.4 us
    unnamed x45, local copies, waits for them, and re-layouts  10.3 us
    all_gather x1, waiting for transfers between devices, per_device(): lax.all_gather(tokens[0].reshape(2 * shard_rows, tokens.shape[3]), 'head'...  8.87 us
  transfers between devices with their start and end apart: 6, of which 6 were waited for; matrix products, arithmetic and copies ran while one was open for 9% of the time, Pallas kernels for 0%

profile of v1, /device:TPU:0, one launch (start us, length us, event | category | flops | bytes accessed | tf_op | source)
XLA Modules:
  0.0 234.7 jit_solution(7636238975362787115)
XLA Ops:
  7.2 0.7 all-gather.7.cloned.1.call-update
  8.0 1.9 pad_maximum_fusion
  10.9 0.9 copy.87
  11.9 0.9 copy.85
  14.0 8.9 %all-gather.7.cloned.1.call-done = bf16[256,4096]{1,0:T(8,128)(2,1)} async-done(((bf16[256,2048]{1,0:T(8,128)(2,1)}), bf16[256,4096]{1,0:T(8,128)(2,1)}) %all-gather.7.cloned.1.call-update) | async-done | bytes 2097168 | tf_op jit(solution)/shard_map/all_gather | solution.py:90
  22.9 49.0 %all-gather.5.cloned.1.call-done = bf16[4096,256]{1,0:T(8,128)(2,1)} async-done(((bf16[1024,256]{1,0:T(8,128)(2,1)}), bf16[4096,256]{1,0:T(8,128)(2,1)}) %all-gather.5.cloned.1.call-update) | async-done | bytes 2097168 | tf_op jit(solution)/shard_map/all_gather | solution.py:97
  71.9 3.0 %fusion.88 = bf16[256,256]{0,1:T(8,128)(2,1)S(1)} fusion(bf16[4096,256]{1,0:T(8,128)(2,1)} %all-gather.5.cloned.1.call-done, bf16[256,4096]{1,0:T(8,128)(2,1)} %all-gather.7.cloned.1.call-done), kind=kOutput, calls=%fused_computation.128 | convolution fusion | flops 536936448 | bytes 4325376 | tf_op jit(solution)/shard_map/dot_general | solution.py:95
  74.9 13.4 %all_gather.19 = bf16[512,256]{0,1:T(8,128)(2,1)S(1)} all-gather(bf16[128,256]{0,1:T(8,128)(2,1)S(1)} %slice.67), channel_id=1, replica_groups=mesh['dp'=4,'context'=4,'head'=2] {'context'}, dimensions={0}, use_global_device_ids=true | all-gather | bytes 327680 | tf_op jit(solution)/shard_map/all_gather | solution.py:157
  88.3 0.8 copy.84
  89.1 0.7 slice_bitcast_fusion.2
  89.8 0.3 fusion.114
  90.2 0.6 copy-done.1
  90.8 0.3 fusion.78
  91.2 2.9 %conditional.4 = (f32[1,8,128]{2,1,0:T(8,128)S(1)}, f32[1,8,128]{2,1,0:T(8,128)S(1)}, f32[1,8,128,128]{3,2,1,0:T(8,128)S(1)}, f32[1,8,128]{2,1,0:T(8,128)S(1)}) conditional(s32[]{:T(128)} %convert_element_type.75, () %tuple.57, (s32[512]{0:T(512)S(1)}, s32[128,512]{0,1:T(8,128)S(1)}, bf16[512,1,128]{0,2,1:T(8,128)(2,1)S(1)}, ...), branch_computations={%region_0.1_spmd, %region_1.4_spmd} | conditional | flops 275452928 | bytes 7919648 | solution.py:153
  91.4 0.5 fusion.4
  91.9 0.5 fusion.6
  92.4 1.7 fusion.7
  94.1 0.6 copy-done.12
  94.7 0.2 divide_bitcast_fusion.1
  95.1 2.9 %conditional.5 = (f32[1,8,128]{2,1,0:T(8,128)S(1)}, f32[1,8,128]{2,1,0:T(8,128)S(1)}, f32[1,8,128,128]{3,2,1,0:T(8,128)S(1)}, f32[1,8,128]{2,1,0:T(8,128)S(1)}) conditional(s32[]{:T(128)} %convert_element_type.75, (f32[1,8,128]{2,1,0:T(8,128)S(1)}, f32[1,8,128]{2,1,0:T(8,128)S(1)}, f32[1,8,128,128]{3,2,1,0:T(8,128)S(1)}) %tuple.59, ...), branch_computations={%region_6.7_spmd, %region_7.10_spmd} | conditional | flops 275581952 | bytes 8460320 | solution.py:154
  95.3 0.5 fusion.23
  95.8 1.7 fusion.26
  97.5 0.5 fusion.25
  98.1 0.2 divide_bitcast_fusion
  98.5 0.2 copy-done.13
  99.0 0.8 broadcast_in_dim.123
  99.8 13.3 %while.20 = (s32[]{:T(128)}, f32[128,1,8,128]{3,0,2,1:T(8,128)}, f32[128,1,8,128]{3,0,2,1:T(8,128)S(1)}, f32[512,256]{1,0:T(8,128)S(1)}, s32[]{:T(128)}, /*index...) while((s32[]{:T(128)}, f32[128,1,8,128]{3,0,2,1:T(8,128)}, ...), condition=%wide.region_15.16_spmd.clone.clone, body=%wide.region_10.15_spmd.clone.clone.sunk | while | flops 1350440704 | bytes 32791988 | solution.py:213
  99.8 0.8 fusion.130
  100.6 0.8 add_select_fusion.3
  101.4 1.0 slice_bitcast_fusion.11
  102.4 4.5 %conditional.12 = (f32[128,1,8,128]{3,0,2,1:T(8,128)S(1)}, f32[512,1,128]{2,0,1:T(8,128)S(1)}, f32[512,1,128]{2,0,1:T(8,128)S(1)}) conditional(s32[]{:T(128)} %convert_element_type.131, () %tuple.123, (s32[512]{0:T(512)S(1)}, s32[128,512]{0,1:T(8,128)S(1)}, bf16[512,1,128]{2,0,1:T(8,128)(2,1)S(1)}, bf16[128,1,8,128]{3,0,2,1:T(8,128)(2,1)}, ...), branch_computations={%region_11.11_spmd, %region_12.12_spmd} | conditional | flops 674889728 | bytes 12331032 | solution.py:197
  102.6 1.5 fusion.45
  104.1 0.4 convolution_bitcast_fusion.2
  104.6 0.4 fusion.46
  105.0 1.4 fusion.48
  106.4 0.5 convolution_bitcast_fusion.1
  106.9 1.9 add.305
  108.8 4.0 %conditional.13 = (f32[128,1,8,128]{3,0,2,1:T(8,128)S(1)}, f32[512,1,128]{2,0,1:T(8,128)S(1)}, f32[512,1,128]{2,0,1:T(8,128)S(1)}) conditional(s32[]{:T(128)} %convert_element_type.131, () %tuple.125, (s32[512]{0:T(512)S(1)}, s32[128,512]{0,1:T(8,128)S(1)}, bf16[512,1,128]{2,0,1:T(8,128)(2,1)S(1)}, bf16[128,1,8,128]{3,0,2,1:T(8,128)(2,1)}, ...), branch_computations={%region_13.13_spmd, %region_14.14_spmd} | conditional | flops 674889728 | bytes 13379636 | solution.py:198
  108.9 1.5 fusion.61
  110.5 0.4 convolution_bitcast_fusion.5
  110.9 0.4 fusion.62
  111.4 0.5 copy-done.3
  111.8 0.4 fusion.64
  112.3 0.5 convolution_bitcast_fusion.4
  113.3 0.8 copy.127
  114.2 1.4 fusion.87
  115.6 0.2 fusion.91
  115.9 0.2 fusion.90
  116.1 16.7 %reduce-scatter.10.cloned.1.call-done = bf16[128,256]{1,0:T(8,128)(2,1)} async-done(((bf16[512,256]{1,0:T(8,128)(2,1)}), bf16[128,256]{1,0:T(8,128)(2,1)}) %reduce-scatter.10.cloned.1.call-update) | async-done | bytes 65552
  132.8 0.9 copy.128
  133.7 3.7 %fusion.77 = bf16[4096,256]{0,1:T(8,128)(2,1)} fusion(bf16[256,4096]{1,0:T(8,128)(2,1)} %all-gather.7.cloned.1.call-done, bf16[128,128]{0,1:T(8,128)(2,1)S(1)} %fusion.90, bf16[128,128]{0,1:T(8,128)(2,1)S(1)} %fusion.91, bf16[128,256]{0,1:T(8,128)(2,1)S(1)} %copy.128), kind=kOutput, calls=%fused_computation.112 | convolution fusion | flops 538312704 | bytes 4325376 | tf_op jit(solution)/shard_map/tr,tc->rc/dot_general | solution.py:246
  137.5 41.9 %reduce-scatter.8.cloned.1.call-done = bf16[1024,256]{0,1:T(8,128)(2,1)} async-done(((bf16[4096,256]{0,1:T(8,128)(2,1)}), bf16[1024,256]{0,1:T(8,128)(2,1)}) %reduce-scatter.8.cloned.1.call-update) | async-done | bytes 524304 | tf_op jit(solution)/shard_map/reduce_scatter | solution.py:245
  179.5 2.1 convolution_convert_fusion.1
  181.6 1.0 copy-done
  182.7 0.2 copy.89
  183.1 0.2 copy.93
  183.3 1.0 fusion.84
  184.4 0.8 maximum_bitcast_fusion
  185.3 30.3 %all-gather.9.cloned.1.call-done = bf16[4096,256]{0,1:T(8,128)(2,1)} async-done(((bf16[1024,256]{0,1:T(8,128)(2,1)}), bf16[4096,256]{0,1:T(8,128)(2,1)}) %all-gather.9.cloned.1.call-update) | async-done | bytes 2097168 | tf_op jit(solution)/shard_map/all_gather | solution.py:12
  215.5 3.3 %reshape.438 = bf16[4,1024,256]{1,0,2:T(4,128)(2,1)S(1)} reshape(bf16[4096,256]{0,1:T(8,128)(2,1)} %all-gather.9.cloned.1.call-done) | data formatting | bytes 4194304 | tf_op jit(solution)/shard_map/all_gather | solution.py:12
  218.9 2.8 %reduce_sum.47 = bf16[1024,256]{0,1:T(8,128)(2,1)S(1)} reduce(bf16[4,1024,256]{1,0,2:T(4,128)(2,1)S(1)} %reshape.438, bf16[]{:T(256)} %constant.139.clone.1), dimensions={0}, to_apply=%region_19.20 | reduce | flops 786432 | bytes 2621442 | tf_op jit(solution)/shard_map/reduce_sum | solution.py:13
  221.8 1.0 copy.100
  222.8 1.0 copy.99
  223.8 4.0 %reduce-scatter.6.cloned.1.call-done = bf16[256,2048]{1,0:T(8,128)(2,1)} async-done(((bf16[256,4096]{1,0:T(8,128)(2,1)}), bf16[256,2048]{1,0:T(8,128)(2,1)}) %reduce-scatter.6.cloned.1.call-update) | async-done | bytes 1048592 | tf_op jit(solution)/shard_map/reduce_scatter | solution.py:241
  (81 shorter events, 4.2 us)
Async XLA Ops:
  7.2 3.5 %copy-start.9 = (bf16[1,2,128,1024]{3,2,1,0:T(8,128)(2,1)S(1)}, bf16[1,2,128,1024]{3,2,1,0:T(8,128)(2,1)}, u32[]{:S(2)}) copy-start(bf16[1,2,128,1024]{3,2,1,0:T(8,128)(2,1)} %param.17) | copy-start | bytes 1572868
  7.2 15.7 %all-gather.7.cloned.1.call-start = ((), (), s32[]{:S(2)}) async-start(), calls=%async_computation.4 | async-start | bytes 3145728 | tf_op jit(solution)/shard_map/all_gather | solution.py:90
  7.9 64.0 %all-gather.5.cloned.1.call-start = ((), (), s32[]{:S(2)}) async-start(), calls=%async_computation.3 | async-start | bytes 2621440 | tf_op jit(solution)/shard_map/all_gather | solution.py:97
  9.8 2.9 %copy-start.10 = (bf16[1,2,128,1024]{3,2,1,0:T(8,128)(2,1)S(1)}, bf16[1,2,128,1024]{3,2,1,0:T(8,128)(2,1)}, u32[]{:S(2)}) copy-start(bf16[1,2,128,1024]{3,2,1,0:T(8,128)(2,1)} %param.18) | copy-start | bytes 1572868
  9.9 122.9 %reduce-scatter.10.cloned.1.call-start = ((), (), s32[]{:S(2)}) async-start(), calls=%async_computation.8 | async-start | bytes 327680
  10.8 84.3 %copy-start.4 = (bf16[1,1,128,1024]{2,3,1,0:T(8,128)(2,1)}, bf16[1,1,128,1024]{2,3,1,0:T(8,128)(2,1)S(1)}, u32[]{:S(2)}) copy-start(bf16[1,1,128,1024]{2,3,1,0:T(8,128)(2,1)S(1)} %copy.131) | copy-start | bytes 786436
  13.0 85.9 %copy-start.6 = (bf16[1,1,128,1024]{2,3,1,0:T(8,128)(2,1)}, bf16[1,1,128,1024]{2,3,1,0:T(8,128)(2,1)S(1)}, u32[]{:S(2)}) copy-start(bf16[1,1,128,1024]{2,3,1,0:T(8,128)(2,1)S(1)} %copy.132) | copy-start | bytes 786436
  74.8 16.4 %copy-start.11 = (bf16[256,256]{0,1:T(8,128)(2,1)}, bf16[256,256]{0,1:T(8,128)(2,1)S(1)}, u32[]{:S(2)}) copy-start(bf16[256,256]{0,1:T(8,128)(2,1)S(1)} %fusion.88) | copy-start | bytes 393220
  90.1 0.8 copy-start.1
  94.1 0.6 copy-start.12
  94.1 0.6 copy-start.14
  98.1 0.7 copy-start.13
  98.1 0.7 copy-start.15
  110.9 1.0 copy-start.3
  113.1 2.5 %copy-start.5 = (bf16[1,1,128,1024]{2,3,1,0:T(8,128)(2,1)S(1)}, bf16[1,1,128,1024]{2,3,1,0:T(8,128)(2,1)}, u32[]{:S(2)}) copy-start(bf16[1,1,128,1024]{2,3,1,0:T(8,128)(2,1)} %copy-done.4) | copy-start | bytes 786436
  113.1 2.7 %copy-start.2 = (f32[1,8,128,128]{2,3,1,0:T(8,128)S(1)}, f32[1,8,128,128]{2,3,1,0:T(8,128)}, u32[]{:S(2)}) copy-start(f32[1,8,128,128]{2,3,1,0:T(8,128)} %copy-done.1) | copy-start | bytes 1572868
  113.1 2.7 %copy-start.7 = (bf16[1,1,128,1024]{2,3,1,0:T(8,128)(2,1)S(1)}, bf16[1,1,128,1024]{2,3,1,0:T(8,128)(2,1)}, u32[]{:S(2)}) copy-start(bf16[1,1,128,1024]{2,3,1,0:T(8,128)(2,1)} %copy-done.6) | copy-start | bytes 786436
  114.1 65.3 %reduce-scatter.8.cloned.1.call-start = ((), (), s32[]{:S(2)}) async-start(), calls=%async_computation.6 | async-start | bytes 2621440 | tf_op jit(solution)/shard_map/reduce_scatter | solution.py:245
  137.4 42.1 %copy-start.8 = (bf16[4096,256]{1,0:T(8,128)(2,1)S(1)}, bf16[4096,256]{1,0:T(8,128)(2,1)}, u32[]{:S(2)}) copy-start(bf16[4096,256]{1,0:T(8,128)(2,1)} %all-gather.5.cloned.1.call-done) | copy-start | bytes 6291460
  137.4 78.1 %all-gather.9.cloned.1.call-start = ((), (), s32[]{:S(2)}) async-start(), calls=%async_computation.7 | async-start | bytes 2621440 | tf_op jit(solution)/shard_map/all_gather | solution.py:12
  179.5 48.4 %reduce-scatter.6.cloned.1.call-start = ((), (), s32[]{:S(2)}) async-start(), calls=%async_computation.5 | async-start | bytes 3145728 | tf_op jit(solution)/shard_map/reduce_scatter | solution.py:241
  181.6 1.0 copy-start
Sparse Core Ops, SparseCore 0:
  9.5 13.2 all-gather.6
  25.0 46.8 all-gather.4
  114.3 18.4 reduce-scatter.9
  137.6 41.8 reduce-scatter.7
  181.1 34.3 all-gather.8
  218.2 9.6 reduce-scatter.5
